TPU v7x, 256 devices: a whole 4x4x8 slice. The times are simulated.
256 devices in a mesh: grp: 4 (over y), col: 64 (over x, z, core).
Axes of the slice: x: 4, y: 4, z: 8, core: 2. Of those that a mesh axis runs over, the one named last changes fastest.
Arguments:
- panels: bfloat16 [256, 4, 512, 512], P('col', None, 'grp'), may hold values from -1.296875 to 1.296875
- parent: float32 [256, 512, 512], P('col', 'grp'), may hold values from -6 to 6
- src_block: int32 [64, 40], P('col'), may hold values from 0 to 39, each once within a row
- dest_owner: int32 [2560, 1], P('col'), may hold values from 0 to 63; in each aligned block of 40 rows (0 to 39, 40 to 79, ...) no two rows name the same one
- target: int32 [2560], P('col'), may hold values from 0 to 3
- counts: int32 [64], P('col'), may hold values from 20 to 40, as said below
Outputs:
- assembled: float32 [256, 512, 512], P('col', 'grp')
Inputs may be any that keep to these rules, and one draw needn't show every extreme that they name: `src_block`: each row of a column rank is a permutation of the 40 block pairs. `dest_owner`: among the 40 slots of one column rank at most 1 name the same owner. The live slots of a rank are its first counts[c]; some rank has all 40 live.
All inputs are finite; a program needn't handle non-finite values.
Results may differ from a plain program's by a relative error of at most 0.0026.
Values may be sent and summed in bfloat16 or wider, within the bound.
A program may use at most 128 MiB of HBM per device.

v0:
```python
import jax
import jax.numpy as jnp
import numpy as np
from jax import lax
from jax.sharding import PartitionSpec as P


def place_slots(src_block, dest_owner, target, counts, peer_count, capacity):
    slot_count = src_block.shape[1]
    slot_index = jnp.arange(slot_count, dtype=jnp.int32)
    owner_rank = dest_owner[:, 0]
    matches = (owner_rank[:, None] == jnp.arange(peer_count, dtype=jnp.int32)[None, :]).astype(
        jnp.int32
    )
    earlier = jnp.cumsum(matches, axis=0) - matches
    rank_in = jnp.sum(earlier * matches, axis=1)
    position = owner_rank * capacity + rank_in
    is_live = slot_index < counts[0]
    routed = jnp.zeros((peer_count * capacity,), jnp.int32).at[position].set(target)
    return (src_block[0], position, is_live, routed.reshape(peer_count, capacity))


def pack_updates(flat_updates, chosen, position, is_live, peer_count, capacity):
    picked = flat_updates[chosen]
    picked = jnp.where(is_live[:, None, None], picked, jnp.zeros_like(picked))
    buffer = (
        jnp.zeros((peer_count * capacity,) + picked.shape[1:], picked.dtype)
        .at[position]
        .set(picked)
    )
    return buffer.reshape((peer_count, capacity) + picked.shape[1:])


def assemble(received, labels, targets):
    arrived = received.reshape((-1,) + received.shape[2:])
    flat_labels = labels.reshape(-1)
    select = (flat_labels[None, :] == jnp.arange(targets, dtype=jnp.int32)[:, None]).astype(
        jnp.bfloat16
    )
    return jnp.einsum("tn,nrc->trc", select, arrived, preferred_element_type=jnp.float32)


def pair_products(own_rows, piece_rows):
    blocks = own_rows.shape[1]
    upper_table = np.array([a for a in range(blocks) for b in range(a + 1)], np.int32)
    lower_table = np.array([b for a in range(blocks) for b in range(a + 1)], np.int32)
    left_rows = own_rows[:, upper_table]
    right_rows = piece_rows[:, lower_table]
    return jnp.einsum(
        "fprw,fpcw->fprc", left_rows, right_rows, preferred_element_type=jnp.float32
    ).astype(jnp.bfloat16)


def per_device(panels, parent, src_block, dest_owner, target, counts):
    fronts, blocks, quarter, _ = panels.shape
    pair_count = blocks * (blocks + 1) // 2
    peer_count = lax.axis_size("col")
    slot_count = src_block.shape[1]
    capacity = (slot_count + peer_count - 1) // peer_count + slot_count // (2 * peer_count)
    targets = parent.shape[0]
    chosen, position, is_live, routed = place_slots(
        src_block, dest_owner, target, counts, peer_count, capacity
    )
    products = pair_products(panels, lax.all_gather(panels, "grp", axis=2, tiled=True))
    flat_updates = products.reshape(fronts * pair_count, quarter, products.shape[3])
    buffer = pack_updates(flat_updates, chosen, position, is_live, peer_count, capacity)
    received, labels = (
        lax.all_to_all(buffer, "col", split_axis=0, concat_axis=0, tiled=True),
        lax.all_to_all(routed, "col", split_axis=0, concat_axis=0, tiled=True),
    )
    return parent - assemble(received, labels, targets)


def solution(mesh):
    placed = (
        P("col", None, "grp", None),
        P("col", "grp", None),
        P("col", None),
        P("col", None),
        P("col"),
        P("col"),
    )
    return jax.shard_map(
        per_device, mesh=mesh, in_specs=placed, out_specs=P("col", "grp", None), check_vma=False
    )
```

profile of v0, /device:TPU:24, one launch (start us, length us, event | category | flops | bytes accessed | tf_op | source)
XLA Modules:
  0.0 387.4 jit_solution(11302547754613624316)
XLA Ops:
  6.5 0.0 copy-start.1
  6.5 0.0 copy-start.2
  6.5 0.0 all-gather.2.cloned.1.call-start
  6.5 0.7 all-gather.2.cloned.1.call-update
  7.3 0.7 fusion.13
  8.0 0.1 reduce_window_sum.11
  8.1 0.8 select_reduce_fusion
  8.9 0.7 fusion.17
  9.6 0.8 scatter_custom_fusion
  10.4 0.7 copy.36
  11.1 11.9 %all-to-all-start = ((s32[64,1,1]{2,1,0:T(1,128)}), s32[64,1,1]{2,1,0:T(1,128)S(1)}, u32[]{:S(2)}, u32[]{:S(2)}) async-start(s32[64,1,1]{2,1,0:T(1,128)} %copy.36), calls=%async_computation | async-start | bytes 65536 | tf_op jit(solution)/shard_map/all_to_all | solution.py:69
  23.0 0.7 pad_clamp_fusion.2
  23.7 5.7 %gather_fusion = bf16[10,4,128,512]{3,2,1,0:T(8,128)(2,1)} fusion(bf16[4,4,128,512]{3,2,1,0:T(8,128)(2,1)} %param.10, s32[1024]{0:T(1024)S(1)} %pad_clamp_fusion.2), kind=kCustom, calls=%fused_computation | custom fusion | bytes 10485800 | tf_op jit(solution)/shard_map/gather | solution.py:47
  30.1 0.0 copy-done.1
  30.1 0.0 copy-done.2
  30.2 66.1 %all-gather.2.cloned.1.call-done = bf16[4,4,512,512]{3,2,1,0:T(8,128)(2,1)} async-done(((bf16[4,4,128,512]{3,2,1,0:T(8,128)(2,1)}), bf16[4,4,512,512]{3,2,1,0:T(8,128)(2,1)}) %all-gather.2.cloned.1.call-update) | async-done | bytes 8388624 | tf_op jit(solution)/shard_map/all_gather | solution.py:64
  96.3 6.0 %fusion.22 = (bf16[4,4,256,512]{3,2,1,0:T(8,128)(2,1)}, bf16[4,4,256,512]{3,2,1,0:T(8,128)(2,1)}) fusion(bf16[4,4,512,512]{3,2,1,0:T(8,128)(2,1)} %all-gather.2.cloned.1.call-done), kind=kLoop, calls=%fused_computation.37 | loop fusion | bytes 16777216 | tf_op jit(solution)/shard_map/gather | solution.py:48
  102.3 7.6 %gather_fusion.2 = bf16[10,4,256,512]{3,2,1,0:T(8,128)(2,1)} fusion(bf16[4,4,256,512]{3,2,1,0:T(8,128)(2,1)} %get-tuple-element.5, s32[1024]{0:T(1024)S(1)} %pad_clamp_fusion.1), kind=kCustom, calls=%fused_computation.2 | custom fusion | bytes 20971560 | tf_op jit(solution)/shard_map/gather | solution.py:48
  109.9 0.0 slice-start
  109.9 7.7 %gather_fusion.3 = bf16[10,4,256,512]{3,2,1,0:T(8,128)(2,1)} fusion(bf16[4,4,256,512]{3,2,1,0:T(8,128)(2,1)} %get-tuple-element.6, s32[1024]{0:T(1024)S(1)} %pad_clamp_fusion.1), kind=kCustom, calls=%fused_computation.3 | custom fusion | bytes 20971560 | tf_op jit(solution)/shard_map/gather | solution.py:48
  117.6 0.0 slice-start.1
  117.6 12.3 %copy_bitcast_fusion = (bf16[4,10,256,512]{3,2,1,0:T(8,128)(2,1)S(1)}, bf16[4,10,256,512]{3,2,1,0:T(8,128)(2,1)}) fusion(bf16[10,4,256,512]{3,2,1,0:T(8,128)(2,1)} %gather_fusion.3, bf16[10,4,256,512]{3,2,1,0:T(8,128)(2,1)} %gather_fusion.2), kind=kLoop, calls=%fused_computation.10 | loop fusion | bytes 41943040 | tf_op jit(solution)/shard_map/gather | solution.py:48
  129.9 0.0 slice-done
  129.9 0.0 slice-done.1
  129.9 10.5 %fusion.8 = bf16[4,10,128,512]{3,2,1,0:T(8,128)(2,1)} fusion(bf16[4,10,256,512]{3,2,1,0:T(8,128)(2,1)S(1)} %get-tuple-element.7, bf16[4,10,256,512]{3,2,1,0:T(8,128)(2,1)} %get-tuple-element.8, bf16[10,4,128,512]{3,2,1,0:T(8,128)(2,1)S(1)} %bitcast.34), kind=kOutput, calls=%fused_computation.17 | convolution fusion | flops 2728919040 | bytes 31457280 | tf_op jit(solution)/shard_map/fprw,fpcw->fprc/dot_general | solution.py:49
  140.4 7.2 %gather_fusion.1 = bf16[40,128,512]{2,1,0:T(8,128)(2,1)} fusion(bf16[40,128,512]{2,1,0:T(8,128)(2,1)} %bitcast.35, s32[1024]{0:T(1024)S(1)} %pad_clamp_fusion), kind=kCustom, calls=%fused_computation.1 | custom fusion | bytes 10485920 | tf_op jit(solution)/shard_map/gather | solution.py:24
  147.6 5.3 %broadcast_select_fusion = bf16[40,128,512]{2,1,0:T(8,128)(2,1)} fusion(bf16[40,128,512]{2,1,0:T(8,128)(2,1)} %gather_fusion.1, pred[40]{0:T(512)(128)(4,1)S(1)} %iota_compare_fusion.2), kind=kLoop, calls=%fused_computation.16 | loop fusion | flops 2621440 | bytes 10485800 | tf_op jit(solution)/shard_map/jit(_where)/select_n | solution.py:25
  152.9 4.2 %broadcast_in_dim.30 = bf16[64,128,512]{2,1,0:T(8,128)(2,1)} broadcast(bf16[]{:T(256)} %constant.10.clone.1), dimensions={} | broadcast | bytes 8388610 | tf_op jit(solution)/shard_map/broadcast_in_dim | solution.py:27
  157.1 14.1 %scatter_fusion = bf16[64,128,512]{2,1,0:T(8,128)(2,1)} fusion(bf16[64,128,512]{2,1,0:T(8,128)(2,1)} %broadcast_in_dim.30, s32[40]{0:T(128)S(1)} %fusion.17, bf16[40,128,512]{2,1,0:T(8,128)(2,1)} %broadcast_select_fusion), kind=kCustom, calls=%fused_computation.5 | custom fusion | bytes 15728800 | tf_op jit(solution)/shard_map/scatter | solution.py:29
  171.2 0.0 all-to-all-done
  171.2 11.0 %all-to-all-start.1 = ((bf16[64,1,128,512]{3,2,1,0:T(8,128)(2,1)}), bf16[64,1,128,512]{3,2,1,0:T(8,128)(2,1)}, u32[]{:S(2)}, u32[]{:S(2)}) async-start(bf16[64,1,128,512]{3,2,1,0:T(8,128)(2,1)} %bitcast.32), calls=%async_computation.1 | async-start | bytes 16777216 | tf_op jit(solution)/shard_map/all_to_all | solution.py:68
  182.2 0.0 copy-start
  182.3 1.2 reduce
  183.5 183.4 %all-to-all-done.1 = bf16[64,1,128,512]{3,2,1,0:T(8,128)(2,1)} async-done(((bf16[64,1,128,512]{3,2,1,0:T(8,128)(2,1)}), bf16[64,1,128,512]{3,2,1,0:T(8,128)(2,1)}, u32[]{:S(2)}, u32[]{:S(2)}) %all-to-all-start.1) | async-done | bytes 8388640 | tf_op jit(solution)/shard_map/all_to_all | solution.py:68
  366.8 12.3 %fusion.4 = f32[4,128,512]{2,0,1:T(4,128)S(1)} fusion(bf16[64,1,128,512]{3,2,1,0:T(8,128)(2,1)} %all-to-all-done.1, s32[64]{0:T(128)S(1)} %reduce), kind=kOutput, calls=%fused_computation.12 | convolution fusion | flops 33554688 | bytes 9437440 | tf_op jit(solution)/shard_map/tn,nrc->trc/dot_general | solution.py:40
  379.1 0.0 copy-done
  379.1 1.4 copy_subtract_fusion
  (5 shorter events, 0.0 us)
Async XLA Ops:
  6.5 23.6 %copy-start.1 = (s32[10]{0:T(128)S(1)}, s32[10]{0:T(128)}, u32[]{:S(2)}) copy-start(s32[10]{0:T(128)} %constant.35) | copy-start | bytes 124
  6.5 23.6 %copy-start.2 = (s32[1,40]{1,0:T(1,128)S(1)}, s32[1,40]{1,0:T(1,128)}, u32[]{:S(2)}) copy-start(s32[1,40]{1,0:T(1,128)} %param.12) | copy-start | bytes 484
  6.5 89.7 %all-gather.2.cloned.1.call-start = ((), (), s32[]{:S(2)}) async-start(), calls=%async_computation.2 | async-start | bytes 10485760 | tf_op jit(solution)/shard_map/all_gather | solution.py:64
  11.1 160.1 %all-to-all-start = ((s32[64,1,1]{2,1,0:T(1,128)}), s32[64,1,1]{2,1,0:T(1,128)S(1)}, u32[]{:S(2)}, u32[]{:S(2)}) async-start(s32[64,1,1]{2,1,0:T(1,128)} %copy.36), calls=%async_computation | async-start | bytes 65536 | tf_op jit(solution)/shard_map/all_to_all | solution.py:69
  109.9 20.0 %slice-start = ((s8[5242880]{0:T(1024)(128)(4,1)}), s8[1048576]{0:T(1024)(128)(4,1)S(1)}, s32[]{:S(2)}) async-start(s8[5242880]{0:T(1024)(128)(4,1)} %bitcast.33), calls=%async_computation.3 | async-start | bytes 2097152
  117.6 12.4 %slice-start.1 = ((s8[5242880]{0:T(1024)(128)(4,1)}), s8[4194304]{0:T(1024)(128)(4,1)S(1)}, s32[]{:S(2)}) async-start(s8[5242880]{0:T(1024)(128)(4,1)} %bitcast.33), calls=%async_computation.4 | async-start | bytes 8388608
  171.2 195.6 %all-to-all-start.1 = ((bf16[64,1,128,512]{3,2,1,0:T(8,128)(2,1)}), bf16[64,1,128,512]{3,2,1,0:T(8,128)(2,1)}, u32[]{:S(2)}, u32[]{:S(2)}) async-start(bf16[64,1,128,512]{3,2,1,0:T(8,128)(2,1)} %bitcast.32), calls=%async_computation.1 | async-start | bytes 16777216 | tf_op jit(solution)/shard_map/all_to_all | solution.py:68
  182.2 196.9 %copy-start = (f32[4,128,512]{2,1,0:T(8,128)S(1)}, f32[4,128,512]{2,1,0:T(8,128)}, u32[]{:S(2)}) copy-start(f32[4,128,512]{2,1,0:T(8,128)} %param.11) | copy-start | bytes 3145732
Sparse Core Ops, SparseCore 0:
  9.1 87.0 all-gather.1
where the time goes:
time: 391 us; the launch traced here: 387 us
  waiting for transfers between devices  250 us (64%)
  local copies, waits for them, and re-layouts  66.4 us (17%)
  starting transfers between devices  22.9 us (6%)
  matrix products  22.8 us (6%)
  between operations  14.1 us (4%)
  other arithmetic  10.9 us (3%)
    all_to_all x1, waiting for transfers between devices, per_device(): lax.all_to_all(buffer, 'col', split_axis=0, concat_axis=0, tiled=True)  183 us
    all_gather x1, waiting for transfers between devices, per_device(): lax.all_gather(panels, 'grp', axis=2, tiled=True)  66.1 us
    gather x4, local copies, waits for them, and re-layouts, pair_products(): right_rows = piece_rows[:, lower_table]  33.6 us
    scatter x1, local copies, waits for them, and re-layouts, pack_updates(): buffer = jnp.zeros((peer_count * capacity,) + picked.shape[1:], picked.dt...  14.1 us
    dot_general x1, matrix products, assemble(): jnp.einsum('tn,nrc->trc', select, arrived, preferred_element_type=jnp.flo...  12.3 us
    all_to_all x1, starting transfers between devices, per_device(): lax.all_to_all(routed, 'col', split_axis=0, concat_axis=0, tiled=True)  11.9 us
    all_to_all x1, starting transfers between devices, per_device(): lax.all_to_all(buffer, 'col', split_axis=0, concat_axis=0, tiled=True)  11 us
    dot_general x1, matrix products, pair_products(): jnp.einsum('fprw,fpcw->fprc', left_rows, right_rows, preferred_element_ty...  10.5 us
  transfers between devices with their start and end apart: 3, of which 2 were waited for; matrix products, arithmetic and copies ran while one was open for 22% of the time, Pallas kernels for 0%

commit v1 on v0

v1 whole, which is shorter than its diff:
```python
import jax
import jax.numpy as jnp
import numpy as np
from jax import lax
from jax.experimental import pallas as pl
from jax.experimental.pallas import tpu as pltpu
from jax.sharding import PartitionSpec as P

MESH = pl.DeviceIdType.MESH
NX, NZ, NY = 4, 8, 4
CHUNKS = 8
HR = 32
LANES = 128
UPPER = np.array([a for a in range(4) for b in range(a + 1)], np.int32)
LOWER = np.array([b for a in range(4) for b in range(a + 1)], np.int32)


def assemble_kernel(
    tab, panels, lab, parent, out,
    u0, u1, u2, u3, d0, d1, d2, d3,
    sendb, rx1, rlab, zsp, zrp, zsm, zrm, x2s, x2r, fin, yra, yrb, yrc,
    y_ss, y_rs, l_ss, l_rs, x1_ss, x1_rs, z_ss, z_rs, x2_ss, x2_rs, f_ss, f_rs,
):
    ups, downs = (u0, u1, u2, u3), (d0, d1, d2, d3)
    y = lax.axis_index("grp")
    col = lax.axis_index("col")
    core = lax.rem(col, 2)
    z = lax.rem(col // 2, NZ)
    x = col // (2 * NZ)

    def dev(yy, xx, zz, cc):
        return (lax.rem(yy + NY, NY), (lax.rem(xx + NX, NX) * NZ + lax.rem(zz + NZ, NZ)) * 2 + cc)

    sib = dev(y, x, z, 1 - core)
    s_of = [1 - 2 * lax.rem(x + h, 2) for h in range(2)]
    partner = [(dev(y, x + s, z, core), dev(y, x + s, z, 1 - core)) for s in s_of]
    second = [dev(y, x - s, z, core) for s in s_of]
    z_up, z_dn = dev(y, x, z + 1, core), dev(y, x, z - 1, core)
    y_up, y_dn = dev(y + 1, x, z, core), dev(y - 1, x, z, core)

    barrier = pltpu.get_barrier_semaphore()
    peers = [sib, partner[0][0], partner[0][1], partner[1][0], partner[1][1], z_up, z_dn, y_up, y_dn]
    for peer in peers:
        pl.semaphore_signal(barrier, inc=1, device_id=peer, device_id_type=MESH)
    pl.semaphore_wait(barrier, len(peers))

    def rcopy(src, dst, ss, rs, who):
        return pltpu.make_async_remote_copy(
            src_ref=src, dst_ref=dst, send_sem=ss, recv_sem=rs, device_id=who, device_id_type=MESH
        )

    def y_copy(q, side):
        dst = (ups if side == 0 else downs)[q]
        return rcopy(panels.at[:, q * HR:(q + 1) * HR, :], dst, y_ss.at[q, side], y_rs.at[q, side],
                     y_dn if side == 0 else y_up)

    def x1_who(h, k):
        return (sib, partner[h][0], partner[h][1])[k]

    def lab_copy(h, k):
        return rcopy(lab.at[h, k + 1], rlab.at[h, k], l_ss.at[h, k], l_rs.at[h, k], x1_who(h, k))

    def x1_copy(c, h, k):
        return rcopy(sendb.at[c, h, k + 1], rx1.at[c, h, k], x1_ss.at[c, h, k], x1_rs.at[c, h, k], x1_who(h, k))

    def z_first(c, side):
        src, dst, who = ((zsp, zrp, z_up), (zsm, zrm, z_dn))[side]
        return rcopy(src.at[c, 0, side], dst.at[c, 0, side], z_ss.at[c, 0, side], z_rs.at[c, 0, side], who)

    def z_copy(c, s, side):
        src, dst, who = ((zsp, zrp, z_up), (zsm, zrm, z_dn))[side]
        return rcopy(src.at[c, s], dst.at[c, s], z_ss.at[c, s, side], z_rs.at[c, s, side], who)

    def x2_copy(c, h):
        return rcopy(x2s.at[c, h], x2r.at[c, h], x2_ss.at[c, h], x2_rs.at[c, h], second[h])

    def f_copy_a(q):
        return rcopy(fin.at[2 + q, 0], yra.at[q], f_ss.at[q, 0], f_rs.at[q, 0], y_up)

    def f_copy_b(q):
        return rcopy(fin.at[2 + q, 1], yrb.at[q], f_ss.at[q, 1], f_rs.at[q, 1], y_dn)

    def f_copy_c(q):
        return rcopy(fin.at[6 + q], yrc.at[q], f_ss.at[4 + q, 0], f_rs.at[4 + q, 0], y_dn)

    for h in range(2):
        for k in range(3):
            lab_copy(h, k).start()
    for q in range(4):
        for side in range(2):
            y_copy(q, side).start()

    def multiply(c, part, left, right):
        def one(j, carry):
            n = part * 16 + j
            xo, zo, co = n // 16, lax.rem(n // 2, NZ), lax.rem(n, 2)
            ia, ib = tab[2 * n], tab[2 * n + 1]
            block = lax.dot_general(
                left(ia), right(ib), (((1,), (1,)), ((), ())), preferred_element_type=jnp.float32
            ).astype(jnp.bfloat16)
            cc = lax.rem(co + core, 2)
            for h in range(2):
                e = lax.rem((xo - x) * s_of[h] + 9, 4)
                sendb[c, h, (e // 2) * 2 + cc, zo * 2 + lax.rem(e, 2)] = block[h * HR:(h + 1) * HR]
            return carry

        lax.fori_loop(0, 16, one, 0, unroll=4)

    def products(c, part):
        own = lambda i: panels[i]

        for k in range(2):
            @pl.when(c == k)
            def _():
                multiply(c, part, lambda i: panels[i, k * 64:(k + 1) * 64, :], own)

        for q in range(4):
            @pl.when(c == 2 + q)
            def _():
                @pl.when(part == 0)
                def _():
                    y_copy(q, 0).wait_recv()
                    y_copy(q, 1).wait_recv()

                multiply(c, part, lambda i: jnp.concatenate([ups[q][i], downs[q][i]], axis=0), own)

        for k in range(2):
            @pl.when(c == 6 + k)
            def _():
                multiply(
                    c, part,
                    lambda i: jnp.concatenate([downs[2 * k][i], downs[2 * k + 1][i]], axis=0),
                    lambda i: jnp.concatenate([u[i] for u in ups], axis=0),
                )

    def x1_send(c):
        for h in range(2):
            for k in range(3):
                x1_copy(c, h, k).start()

    def local_sum(c, h, d, i, base):
        rows = d * 2 + i
        flip = d * 2 + (1 - i)
        blocks = [sendb[c, h, 0, rows], rx1[c, h, 0, rows], rx1[c, h, 1, flip], rx1[c, h, 2, flip]]
        labels = [lab[h, 0, pl.ds(rows, 1), :], rlab[h, 0, pl.ds(rows, 1), :],
                  rlab[h, 1, pl.ds(flip, 1), :], rlab[h, 2, pl.ds(flip, 1), :]]
        blocks = [b.astype(jnp.float32) for b in blocks]
        labels = [jnp.broadcast_to(v, (HR, LANES)) for v in labels]
        sums = []
        for t in range(4):
            total = None if base is None else base[t]
            for b, v in zip(blocks, labels):
                term = jnp.where(v == t + 1, b, 0.0)
                total = term if total is None else total + term
            sums.append(total)
        return sums

    def merge(c, s, h, d, prev, dst):
        for i in range(2):
            base = None if prev is None else [prev[c, s - 1, h, i * 4 + t].astype(jnp.float32) for t in range(4)]
            for t, v in enumerate(local_sum(c, h, d, i, base)):
                dst[c, s, h, i * 4 + t] = v.astype(jnp.bfloat16)

    def z_step(c, s):
        dp, dm = lax.rem(z + 4 - s, NZ), lax.rem(z + 4 + s, NZ)

        @pl.when(s == 0)
        def _():
            @pl.when(c == 0)
            def _():
                for h in range(2):
                    for k in range(3):
                        lab_copy(h, k).wait_recv()
            for h in range(2):
                for k in range(3):
                    x1_copy(c, h, k).wait_recv()
            merge(c, s, 0, dp, None, zsp)
            z_first(c, 0).start()
            merge(c, s, 1, dm, None, zsm)
            z_first(c, 1).start()

        @pl.when(s == 1)
        def _():
            z_first(c, 0).wait_recv()
            merge(c, s, 0, dp, zrp, zsp)
            merge(c, s, 1, dp, None, zsp)
            z_copy(c, s, 0).start()
            z_first(c, 1).wait_recv()
            merge(c, s, 1, dm, zrm, zsm)
            merge(c, s, 0, dm, None, zsm)
            z_copy(c, s, 1).start()

        @pl.when(s >= 2)
        def _():
            z_copy(c, s - 1, 0).wait_recv()
            for h in range(2):
                merge(c, s, h, dp, zrp, zsp)
            z_copy(c, s, 0).start()
            z_copy(c, s - 1, 1).wait_recv()
            for h in range(2):
                merge(c, s, h, dm, zrm, zsm)
            z_copy(c, s, 1).start()

    def z_last(c):
        z_copy(c, 3, 0).wait_recv()
        z_copy(c, 3, 1).wait_recv()
        for h in range(2):
            for i in range(2):
                base = [zrp[c, 3, h, i * 4 + t].astype(jnp.float32) + zrm[c, 3, h, i * 4 + t].astype(jnp.float32)
                        for t in range(4)]
                for t, v in enumerate(local_sum(c, h, z, i, base)):
                    if i == 0:
                        x2s[c, h, t] = v.astype(jnp.bfloat16)
                    else:
                        fin[c, h, t] = v
            x2_copy(c, h).start()

    def finish(c):
        for h in range(2):
            x2_copy(c, h).wait_recv()
            fin[c, h] = fin[c, h] + x2r[c, h].astype(jnp.float32)
        lanes = pl.ds(pl.multiple_of(y * LANES, LANES), LANES)
        for k in range(2):
            @pl.when(c == k)
            def _():
                for h in range(2):
                    rows = slice(k * 64 + h * HR, k * 64 + (h + 1) * HR)
                    out[:, rows, lanes] = parent[:, rows, lanes] - fin[k, h]

        for q in range(4):
            @pl.when(c == 2 + q)
            def _():
                f_copy_a(q).start()
                f_copy_b(q).start()

        for q in range(2):
            @pl.when(c == 6 + q)
            def _():
                f_copy_c(q).start()

    def first(part, carry):
        products(jnp.int32(0), part)
        return carry

    lax.fori_loop(0, 4, first, 0)
    x1_send(0)

    def tick(t, carry):
        c5 = t - 5

        @pl.when(c5 >= 0)
        def _():
            finish(c5)

        c4 = t - 4

        @pl.when(jnp.logical_and(c4 >= 0, c4 < CHUNKS))
        def _():
            z_last(c4)

        def inner(r, carry):
            s = 3 - r
            c = t - s

            @pl.when(jnp.logical_and(c >= 0, c < CHUNKS))
            def _():
                z_step(c, s)

            @pl.when(t + 1 < CHUNKS)
            def _():
                products(t + 1, r)

            return carry

        lax.fori_loop(0, 4, inner, 0)

        @pl.when(t + 1 < CHUNKS)
        def _():
            x1_send(t + 1)

        return carry

    lax.fori_loop(0, CHUNKS + 5, tick, 0)

    for q in range(4):
        rows = slice(q * HR, (q + 1) * HR)
        f_copy_a(q).wait_recv()
        lanes = pl.ds(pl.multiple_of(lax.rem(y + 3, NY) * LANES, LANES), LANES)
        out[:, rows, lanes] = parent[:, rows, lanes] - yra[q]
        f_copy_b(q).wait_recv()
        lanes = pl.ds(pl.multiple_of(lax.rem(y + 1, NY) * LANES, LANES), LANES)
        out[:, rows, lanes] = parent[:, rows, lanes] - yrb[q]
    for q in range(2):
        f_copy_c(q).wait_recv()
        for h in range(2):
            rows = slice(q * 64 + h * HR, q * 64 + (h + 1) * HR)
            lanes = pl.ds(pl.multiple_of(lax.rem(y + 2, NY) * LANES, LANES), LANES)
            out[:, rows, lanes] = parent[:, rows, lanes] - yrc[q, h]

    for h in range(2):
        for k in range(3):
            lab_copy(h, k).wait_send()
    for q in range(4):
        for side in range(2):
            y_copy(q, side).wait_send()
        f_copy_a(q).wait_send()
        f_copy_b(q).wait_send()
    for q in range(2):
        f_copy_c(q).wait_send()

    def drain(c, carry):
        for h in range(2):
            for k in range(3):
                x1_copy(c, h, k).wait_send()
            x2_copy(c, h).wait_send()
        for side in range(2):
            z_first(c, side).wait_send()
            for s in range(1, 4):
                z_copy(c, s, side).wait_send()
        return carry

    lax.fori_loop(0, CHUNKS, drain, 0)


def tables(src_block, dest_owner, target, counts):
    col = lax.axis_index("col")
    core, x = col % 2, col // (2 * NZ)
    slots = src_block.shape[1]
    live = jnp.arange(slots, dtype=jnp.int32) < counts[0]
    owner = dest_owner[:, 0]
    pair = src_block[0]
    within = pair % 10
    upper = sum((within >= k).astype(jnp.int32) for k in (1, 3, 6))
    lower = within - upper * (upper + 1) // 2
    base = (pair // 10) * 4
    owners = jnp.arange(64, dtype=jnp.int32)
    hit = owners[:, None] == owner[None, :]
    both = jnp.stack([base + upper, base + lower])
    tab = jnp.sum(jnp.where(hit[:, None, :], both[None], 0), axis=2).reshape(-1)
    shape = (2, 2, 2, NZ, 2)
    h, jj, cc, zo, i = [lax.broadcasted_iota(jnp.int32, shape, a) for a in range(5)]
    s = 1 - 2 * ((x + h) % 2)
    xo = (x + s * (jj * 2 + i - 1) + 8) % 4
    named = (xo * NZ + zo) * 2 + (cc + core) % 2
    hit = (named.reshape(-1)[:, None] == owner[None, :]) & live[None, :]
    label = jnp.sum(jnp.where(hit, target[None, :] + 1, 0), axis=1)
    return tab, jnp.broadcast_to(label[:, None], (128, LANES)).reshape(2, 4, 16, LANES)


def per_device(panels, parent, src_block, dest_owner, target, counts):
    tab, lab = tables(src_block, dest_owner, target, counts)
    vmem = pl.BlockSpec(memory_space=pltpu.VMEM)
    bf, f32, i32 = jnp.bfloat16, jnp.float32, jnp.int32
    dma = pltpu.SemaphoreType.DMA
    return pl.pallas_call(
        assemble_kernel,
        out_shape=jax.ShapeDtypeStruct((4, 128, 512), f32),
        in_specs=[pl.BlockSpec(memory_space=pltpu.SMEM), vmem, vmem, vmem],
        out_specs=vmem,
        scratch_shapes=[pltpu.VMEM((16, HR, 512), bf) for _ in range(8)] + [
            pltpu.VMEM((CHUNKS, 2, 4, 16, HR, LANES), bf),
            pltpu.VMEM((CHUNKS, 2, 3, 16, HR, LANES), bf),
            pltpu.VMEM((2, 3, 16, LANES), i32),
            pltpu.VMEM((CHUNKS, 4, 2, 8, HR, LANES), bf),
            pltpu.VMEM((CHUNKS, 4, 2, 8, HR, LANES), bf),
            pltpu.VMEM((CHUNKS, 4, 2, 8, HR, LANES), bf),
            pltpu.VMEM((CHUNKS, 4, 2, 8, HR, LANES), bf),
            pltpu.VMEM((CHUNKS, 2, 4, HR, LANES), bf),
            pltpu.VMEM((CHUNKS, 2, 4, HR, LANES), bf),
            pltpu.VMEM((CHUNKS, 2, 4, HR, LANES), f32),
            pltpu.VMEM((4, 4, HR, LANES), f32),
            pltpu.VMEM((4, 4, HR, LANES), f32),
            pltpu.VMEM((2, 2, 4, HR, LANES), f32),
            dma((4, 2)), dma((4, 2)),
            dma((2, 3)), dma((2, 3)),
            dma((CHUNKS, 2, 3)), dma((CHUNKS, 2, 3)),
            dma((CHUNKS, 4, 2)), dma((CHUNKS, 4, 2)),
            dma((CHUNKS, 2)), dma((CHUNKS, 2)),
            dma((6, 2)), dma((6, 2)),
        ],
        compiler_params=pltpu.CompilerParams(
            collective_id=0, has_side_effects=True, vmem_limit_bytes=60 * 1024 * 1024
        ),
    )(tab, panels.reshape(16, 128, 512), lab, parent)


def solution(mesh):
    placed = (
        P("col", None, "grp", None),
        P("col", "grp", None),
        P("col", None),
        P("col", None),
        P("col"),
        P("col"),
    )
    return jax.shard_map(
        per_device, mesh=mesh, in_specs=placed, out_specs=P("col", "grp", None), check_vma=False
    )
```

time: 391 us -> 135 us (0.35)
  waiting for transfers between devices: 250 us -> 0 us
  Pallas kernels: 0 us -> 126 us
  local copies, waits for them, and re-layouts: 66.4 us -> 4.62 us
  starting transfers between devices: 22.9 us -> 0 us
  matrix products: 22.8 us -> 0 us
  between operations: 14.1 us -> 0.7 us
  other arithmetic: 10.9 us -> 3.72 us
    all_to_all x2 -> x0, waiting for transfers between devices: 183 us -> none  [the longest x1 183 us: per_device(): lax.all_to_all(buffer, 'col', split_axis=0, concat_axis=0, tiled=True)]
    pallas_call x0 -> x1, Pallas kernels: none -> 126 us  [per_device(): pl.pallas_call(assemble_kernel, out_shape=jax.ShapeDtypeStruct((4, 128, 5...]
    all_gather x1 -> x0, waiting for transfers between devices: 66.1 us -> none  [per_device(): lax.all_gather(panels, 'grp', axis=2, tiled=True)]
    gather x6 -> x0, local copies, waits for them, and re-layouts: 46.5 us -> none  [the longest x4 33.6 us: pair_products(): right_rows = piece_rows[:, lower_table]]
    all_to_all x2 -> x0, starting transfers between devices: 22.9 us -> none  [the longest x1 11.9 us: per_device(): lax.all_to_all(routed, 'col', split_axis=0, concat_axis=0, tiled=True)]
    dot_general x2 -> x0, matrix products: 22.8 us -> none  [the longest x1 12.3 us: assemble(): jnp.einsum('tn,nrc->trc', select, arrived, preferred_element_type=jnp.flo...]
    scatter x2 -> x0, local copies, waits for them, and re-layouts: 14.9 us -> none  [the longest x1 14.1 us: pack_updates(): buffer = jnp.zeros((peer_count * capacity,) + picked.shape[1:], picked.dt...]
    select_n x3 -> x0, other arithmetic: 5.95 us -> none  [the longest x1 5.28 us: pack_updates(): picked = jnp.where(is_live[:, None, None], picked, jnp.zeros_like(picked))]
  transfers between devices with their start and end apart: 3 -> 0, of which waited for: 2 -> 0; matrix products, arithmetic and copies ran while one was open for 22% -> 0% of each run, Pallas kernels for 0% -> 0%
where the time goes in v1:
time: 135 us
  Pallas kernels  126 us (93%)
  local copies, waits for them, and re-layouts  4.62 us (3%)
  other arithmetic  3.72 us (3%)
    pallas_call x1, Pallas kernels, per_device(): pl.pallas_call(assemble_kernel, out_shape=jax.ShapeDtypeStruct((4, 128, 5...  126 us

profile of v1, /device:TPU:24, one launch (start us, length us, event | category | flops | bytes accessed | tf_op | source)
XLA Modules:
  0.0 134.7 jit_solution(3799180728948237686)
XLA Ops:
  0.7 0.7 broadcast_add_fusion
  1.3 0.7 fusion.12
  2.0 0.7 subtract_add_fusion
  2.7 0.7 iota_compare_fusion
  3.4 0.1 select_reduce_fusion
  3.5 0.1 copy.7
  3.6 0.7 reshape.129.tab
  4.4 0.1 add_add_fusion
  4.4 0.1 sub.36
  4.6 0.1 iota.51
  4.7 0.1 iota.52
  4.8 0.1 iota.59
  4.9 0.1 iota.60
  5.0 0.1 iota.57
  5.2 0.8 select_reduce_fusion.1
  6.0 0.1 broadcast_in_dim.50
  6.0 0.7 broadcast_in_dim.51.lab
  6.8 125.7 %shard_map.64 = f32[4,128,512]{2,1,0:T(8,128)} custom-call(s32[128]{0:T(128)} %reshape.129.tab, bf16[16,128,512]{2,1,0:T(8,128)(2,1)} %bitcast.12, s32[2,4,16,128]{3,2,1,0:T(8,128)} %broadcast_in_dim.51.lab, f32[4,128,512]{2,1,0:T(8,128)} %parent.1), custom_call_target="tpu_custom_call" | custom-call | tf_op jit(solution)/shard_map/pallas_call | solution.py:355
  132.4 2.3 %copy.10 = f32[4,128,512]{2,1,0:T(8,128)} copy(f32[4,128,512]{2,1,0:T(8,128)} %shard_map.64) | data formatting | bytes 2097152
  (7 shorter events, 0.1 us)

commit v2 on v0

v2 whole, which is shorter than its diff:
```python
import jax
import jax.numpy as jnp
from jax import lax
from jax.experimental import pallas as pl
from jax.experimental.pallas import tpu as pltpu
from jax.sharding import PartitionSpec as P

MESH = pl.DeviceIdType.MESH
NX, NZ, NY = 4, 8, 4
CHUNKS = 16
HR = 16
LANES = 128
EARLY_FROM, EARLY_STEP = 5, 3
EARLY = (CHUNKS - 1 - EARLY_FROM) // EARLY_STEP + 1
EARLY_GAP, LAST_GAP = 2, 2
UNROLL = 8
GROUP_TICK = (None, 1, 3, 5, 7, 8)


def is_early(c):
    return jnp.logical_and(lax.rem(c + EARLY_STEP * CHUNKS - EARLY_FROM, EARLY_STEP) == 0, c >= EARLY_FROM)


def assemble_kernel(
    counts, panels, src, dest, target, out,
    u0, u1, u2, u3, d0, d1, d2, d3,
    own_t, up_t, tabv, tab, lab, sendb, rx1, rlab, zsp, zrp, zsm, zrm, x2s, x2r, x2as, x2ar, fin, fr,
    t_sem, y_ss, y_rs, l_ss, l_rs, x1_ss, x1_rs, z_ss, z_rs, x2_ss, x2_rs, a_ss, a_rs, f_ss, f_rs,
):
    ups, downs = (u0, u1, u2, u3), (d0, d1, d2, d3)
    y = lax.axis_index("grp")
    col = lax.axis_index("col")
    core = lax.rem(col, 2)
    z = lax.rem(col // 2, NZ)
    x = col // (2 * NZ)

    def dev(yy, xx, zz, cc):
        return (lax.rem(yy + NY, NY), (lax.rem(xx + NX, NX) * NZ + lax.rem(zz + NZ, NZ)) * 2 + cc)

    sib = dev(y, x, z, 1 - core)
    s_of = [1 - 2 * lax.rem(x + h, 2) for h in range(2)]
    partner = [(dev(y, x + s, z, core), dev(y, x + s, z, 1 - core)) for s in s_of]
    second = [{dy: dev(y + dy, x - s, z, core) for dy in (-1, 0, 1)} for s in s_of]
    z_up, z_dn = dev(y, x, z + 1, core), dev(y, x, z - 1, core)
    y_side = {1: dev(y + 1, x, z, core), -1: dev(y - 1, x, z, core)}

    barrier = pltpu.get_barrier_semaphore()
    peers = [sib, partner[0][0], partner[0][1], partner[1][0], partner[1][1], z_up, z_dn, y_side[1], y_side[-1],
             second[0][1], second[0][-1], second[1][1], second[1][-1]]
    for peer in peers:
        pl.semaphore_signal(barrier, inc=1, device_id=peer, device_id_type=MESH)

    slots = src.shape[1]
    i32 = jnp.int32
    lane40, row40 = lax.broadcasted_iota(i32, (slots, slots), 1), lax.broadcasted_iota(i32, (slots, slots), 0)

    def column(line):
        return jnp.sum(jnp.where(lane40 == row40, jnp.broadcast_to(line, (slots, slots)), 0), axis=1, keepdims=True)

    def wide(v):
        return jnp.broadcast_to(v, (slots, LANES))

    pair = column(src[...])
    goal = column(target[...])
    front = sum((pair >= 10 * k).astype(i32) for k in (1, 2, 3))
    within = pair - 10 * front
    upper = sum((within >= k).astype(i32) for k in (1, 3, 6))
    lower = within - ((upper * (upper + 1)) >> 1)
    hit = wide(column(dest[...])) == lax.broadcasted_iota(i32, (slots, LANES), 1)
    live = lax.broadcasted_iota(i32, (slots, LANES), 0) < counts[0]

    def pick(value, mask):
        return jnp.sum(jnp.where(mask, wide(value), 0), axis=0, keepdims=True)

    tabv[...] = jnp.broadcast_to(pick((front * 4 + upper) * 16 + front * 4 + lower, hit), (8, LANES))
    tab_copy = pltpu.make_async_copy(tabv, tab, t_sem)
    tab_copy.start()
    label = pick(goal + 1, jnp.logical_and(hit, live))
    place = lax.broadcasted_iota(i32, (LANES, LANES), 0)
    pi, pz, pc, pj, ph = place & 1, (place >> 1) & 7, (place >> 4) & 1, (place >> 5) & 1, place >> 6
    turn = 1 - 2 * ((x + ph) & 1)
    named = (((x + turn * (pj * 2 + pi - 1) + 8) & 3) * NZ + pz) * 2 + ((pc + core) & 1)
    labels = jnp.sum(
        jnp.where(named == lax.broadcasted_iota(i32, (LANES, LANES), 1), jnp.broadcast_to(label, (LANES, LANES)), 0),
        axis=1, keepdims=True,
    )
    lab[...] = jnp.broadcast_to(labels, (LANES, LANES)).reshape(2, 4, 16, LANES)

    pl.semaphore_wait(barrier, len(peers))

    def rcopy(src, dst, ss, rs, who):
        return pltpu.make_async_remote_copy(
            src_ref=src, dst_ref=dst, send_sem=ss, recv_sem=rs, device_id=who, device_id_type=MESH
        )

    def y_copy(q, side):
        dst = (ups if side == 0 else downs)[q]
        return rcopy(panels.at[:, q * 32:(q + 1) * 32, :], dst, y_ss.at[q, side], y_rs.at[q, side],
                     y_side[-1] if side == 0 else y_side[1])

    def x1_who(h, k):
        return (sib, partner[h][0], partner[h][1])[k]

    def lab_copy(h, k):
        return rcopy(lab.at[h, k + 1], rlab.at[h, k], l_ss.at[h, k], l_rs.at[h, k], x1_who(h, k))

    def x1_copy(c, h, k):
        return rcopy(sendb.at[c, h, k + 1], rx1.at[c, h, k], x1_ss.at[c, h, k], x1_rs.at[c, h, k], x1_who(h, k))

    def z_copy(c, s, side, early):
        src, dst, who = ((zsp, zrp, z_up), (zsm, zrm, z_dn))[side]
        if s is None:
            s, h = 0, pl.ds(side, 1)
        else:
            h = pl.ds(0, 2)
        blocks = pl.ds(4, 4) if early else pl.ds(0, 8)
        return rcopy(src.at[c, s, h, blocks], dst.at[c, s, h, blocks], z_ss.at[c, s, side], z_rs.at[c, s, side], who)

    def a_copy(a, h):
        return rcopy(x2as.at[a, h], x2ar.at[a, h], a_ss.at[a, h], a_rs.at[a, h], second[h][0])

    def x2_copy(c, h, dy):
        return rcopy(x2s.at[c, h], x2r.at[c, h], x2_ss.at[c, h], x2_rs.at[c, h], second[h][dy])

    def f_copy(c, h, dy):
        return rcopy(fin.at[c, h], fr.at[c, h], f_ss.at[c, h], f_rs.at[c, h], y_side[dy])

    def turn_block(src, dst):
        def one(i, carry):
            dst[i] = src(i).T
            return carry

        lax.fori_loop(0, 16, one, 0)

    for q in range(4):
        for side in range(2):
            y_copy(q, side).start()
    for h in range(2):
        for k in range(3):
            lab_copy(h, k).start()
    turn_block(lambda i: panels[i], own_t)
    tab_copy.wait()

    def multiply(chunks, left, right):
        def one(n, carry):
            xo, zo, co = n // 16, lax.rem(n // 2, NZ), lax.rem(n, 2)
            both = tab[0, n]
            block = jnp.dot(left(both >> 4), right[both & 15], preferred_element_type=jnp.float32).astype(jnp.bfloat16)
            cc = lax.rem(co + core, 2)
            for h in range(2):
                e = lax.rem((xo - x) * s_of[h] + 9, 4)
                for k, c in enumerate(chunks):
                    r = (h * len(chunks) + k) * HR
                    sendb[c, h, (e // 2) * 2 + cc, zo * 2 + lax.rem(e, 2)] = block[r:r + HR]
            return carry

        lax.fori_loop(0, 64, one, 0, unroll=UNROLL)
        for c in chunks:
            x1_send(c)

    def group(k):
        if k == 0:
            multiply((0, 1, 2, 3), lambda i: panels[i], own_t)
        elif k < 5:
            y_copy(k - 1, 0).wait_recv()
            y_copy(k - 1, 1).wait_recv()
            multiply((2 * k + 2, 2 * k + 3), lambda i: jnp.concatenate([ups[k - 1][i], downs[k - 1][i]], axis=0), own_t)
        else:
            turn_block(lambda i: jnp.concatenate([u[i] for u in ups], axis=0), up_t)
            multiply((12, 13, 14, 15), lambda i: jnp.concatenate([d[i] for d in downs], axis=0), up_t)

    def x1_send(c):
        for h in range(2):
            for k in range(3):
                x1_copy(c, h, k).start()

    def x1_wait(c):
        @pl.when(c == 0)
        def _():
            for h in range(2):
                for k in range(3):
                    lab_copy(h, k).wait_recv()

        for h in range(2):
            for k in range(3):
                x1_copy(c, h, k).wait_recv()

    def local_sum(c, h, d, i, base):
        rows = d * 2 + i
        flip = d * 2 + (1 - i)
        blocks = [sendb[c, h, 0, rows], rx1[c, h, 0, rows], rx1[c, h, 1, flip], rx1[c, h, 2, flip]]
        labels = [lab[h, 0, pl.ds(rows, 1), :], rlab[h, 0, pl.ds(rows, 1), :],
                  rlab[h, 1, pl.ds(flip, 1), :], rlab[h, 2, pl.ds(flip, 1), :]]
        blocks = [b.astype(jnp.float32) for b in blocks]
        labels = [jnp.broadcast_to(v, (HR, LANES)) for v in labels]
        sums = []
        for t in range(4):
            total = None if base is None else base[t]
            for b, v in zip(blocks, labels):
                term = jnp.where(v == t + 1, b, 0.0)
                total = term if total is None else total + term
            sums.append(total)
        return sums

    def plus(a, b):
        return b if a is None else [u + v for u, v in zip(a, b)]

    def early_base(c, h, d):
        return [x2ar[(c - EARLY_FROM) // EARLY_STEP, h, d * 4 + t].astype(jnp.float32) for t in range(4)]

    def merge(c, s, h, d, prev, dst, early):
        for i in (1,) if early else (0, 1):
            base = early_base(c, h, d) if early else None
            if prev is not None:
                base = plus(base, [prev[c, s - 1, h, i * 4 + t].astype(jnp.float32) for t in range(4)])
            for t, v in enumerate(local_sum(c, h, d, i, base)):
                dst[c, s, h, i * 4 + t] = v.astype(jnp.bfloat16)

    def z_step(c, s, early):
        dp, dm = lax.rem(z + 4 - s, NZ), lax.rem(z + 4 + s, NZ)

        @pl.when(s == 0)
        def _():
            if early:
                for h in range(2):
                    a_copy((c - EARLY_FROM) // EARLY_STEP, h).wait_recv()
            else:
                x1_wait(c)
            merge(c, s, 0, dp, None, zsp, early)
            z_copy(c, None, 0, early).start()
            merge(c, s, 1, dm, None, zsm, early)
            z_copy(c, None, 1, early).start()

        @pl.when(s == 1)
        def _():
            z_copy(c, None, 0, early).wait_recv()
            merge(c, s, 0, dp, zrp, zsp, early)
            merge(c, s, 1, dp, None, zsp, early)
            z_copy(c, s, 0, early).start()
            z_copy(c, None, 1, early).wait_recv()
            merge(c, s, 1, dm, zrm, zsm, early)
            merge(c, s, 0, dm, None, zsm, early)
            z_copy(c, s, 1, early).start()

        @pl.when(s >= 2)
        def _():
            z_copy(c, s - 1, 0, early).wait_recv()
            for h in range(2):
                merge(c, s, h, dp, zrp, zsp, early)
            z_copy(c, s, 0, early).start()
            z_copy(c, s - 1, 1, early).wait_recv()
            for h in range(2):
                merge(c, s, h, dm, zrm, zsm, early)
            z_copy(c, s, 1, early).start()

    def places(c, fn):
        p, sub = c // 2, lax.rem(c, 2)

        def lanes(k):
            return pl.ds(pl.multiple_of(lax.rem(y + k, NY) * LANES, LANES), LANES)

        @pl.when(p < 2)
        def _():
            for h in range(2):
                fn(h, 0, h * 64 + c * HR, lanes(0))

        @pl.when(jnp.logical_and(p >= 2, p < 6))
        def _():
            for h in range(2):
                fn(h, 1 - 2 * h, (p - 2) * 32 + sub * HR, lanes(3 if h == 0 else 1))

        @pl.when(p >= 6)
        def _():
            for h in range(2):
                fn(h, -1, h * 64 + (c - 12) * HR, lanes(2))

    def z_last(c, early):
        z_copy(c, 3, 0, early).wait_recv()
        z_copy(c, 3, 1, early).wait_recv()
        for h in range(2):
            for i in (1,) if early else (0, 1):
                base = early_base(c, h, z) if early else None
                for buf in (zrp, zrm):
                    base = plus(base, [buf[c, 3, h, i * 4 + t].astype(jnp.float32) for t in range(4)])
                for t, v in enumerate(local_sum(c, h, z, i, base)):
                    if i == 0:
                        x2s[c, h, t] = v.astype(jnp.bfloat16)
                    else:
                        fin[c, h, t] = v

        def send(h, dy, row, lanes):
            if not early:
                x2_copy(c, h, dy).start()
            if dy != 0:
                f_copy(c, h, dy).start()

        places(c, send)

    def finish(c, early):
        def write(h, dy, row, lanes):
            if not early:
                x2_copy(c, h, dy).wait_recv()
            if dy != 0:
                f_copy(c, h, dy).wait_recv()
            value = (fin if dy == 0 else fr)[c, h]
            if not early:
                value = value + x2r[c, h].astype(jnp.float32)
            out[:, pl.ds(pl.multiple_of(row, HR), HR), lanes] = value

        places(c, write)

    def early_exchange(c):
        x1_wait(c)
        for h in range(2):
            def one(d, carry):
                for t, v in enumerate(local_sum(c, h, d, 0, None)):
                    x2as[(c - EARLY_FROM) // EARLY_STEP, h, d * 4 + t] = v.astype(jnp.bfloat16)
                return carry

            lax.fori_loop(0, NZ, one, 0)
            a_copy((c - EARLY_FROM) // EARLY_STEP, h).start()

    group(0)

    def within(c, early):
        inside = jnp.logical_and(c >= 0, c < CHUNKS)
        return jnp.logical_and(inside, is_early(c) if early else jnp.logical_not(is_early(c)))

    def tick(t, carry):
        @pl.when(within(t, True))
        def _():
            early_exchange(t)

        def inner(s, carry):
            for early in (False, True):
                c = t - s - EARLY_GAP * early

                @pl.when(within(c, early))
                def _():
                    z_step(c, s, early)

            return carry

        lax.fori_loop(0, 4, inner, 0)

        for early in (False, True):
            done = t - 4 - EARLY_GAP * early

            @pl.when(within(done, early))
            def _():
                z_last(done, early)

            @pl.when(within(done - LAST_GAP, early))
            def _():
                finish(done - LAST_GAP, early)

        for k in range(1, 6):
            @pl.when(t == GROUP_TICK[k])
            def _():
                group(k)

        return carry

    lax.fori_loop(0, CHUNKS + 4 + EARLY_GAP + LAST_GAP, tick, 0)

    for h in range(2):
        for k in range(3):
            lab_copy(h, k).wait_send()
        for a in range(EARLY):
            a_copy(a, h).wait_send()
    for q in range(4):
        for side in range(2):
            y_copy(q, side).wait_send()

    def drain(c, carry):
        for h in range(2):
            for k in range(3):
                x1_copy(c, h, k).wait_send()
        for early in (False, True):
            @pl.when(within(c, early))
            def _():
                for side in range(2):
                    z_copy(c, None, side, early).wait_send()
                    for s in range(1, 4):
                        z_copy(c, s, side, early).wait_send()

                def sent(h, dy, row, lanes):
                    if not early:
                        x2_copy(c, h, dy).wait_send()
                    if dy != 0:
                        f_copy(c, h, dy).wait_send()

                places(c, sent)
        return carry

    lax.fori_loop(0, CHUNKS, drain, 0)


def per_device(panels, parent, src_block, dest_owner, target, counts):
    vmem = pl.BlockSpec(memory_space=pltpu.VMEM)
    bf, f32, i32 = jnp.bfloat16, jnp.float32, jnp.int32
    dma = pltpu.SemaphoreType.DMA
    ring = (CHUNKS, 4, 2, 8, HR, LANES)
    tail = (CHUNKS, 2, 4, HR, LANES)
    sums = pl.pallas_call(
        assemble_kernel,
        out_shape=jax.ShapeDtypeStruct((4, 128, 512), f32),
        in_specs=[pl.BlockSpec(memory_space=pltpu.SMEM), vmem, vmem, vmem, vmem],
        out_specs=vmem,
        scratch_shapes=[pltpu.VMEM((16, 32, 512), bf) for _ in range(8)] + [
            pltpu.VMEM((16, 512, 128), bf),
            pltpu.VMEM((16, 512, 128), bf),
            pltpu.VMEM((8, LANES), i32),
            pltpu.SMEM((8, LANES), i32),
            pltpu.VMEM((2, 4, 16, LANES), i32),
            pltpu.VMEM((CHUNKS, 2, 4, 16, HR, LANES), bf),
            pltpu.VMEM((CHUNKS, 2, 3, 16, HR, LANES), bf),
            pltpu.VMEM((2, 3, 16, LANES), i32),
            pltpu.VMEM(ring, bf), pltpu.VMEM(ring, bf), pltpu.VMEM(ring, bf), pltpu.VMEM(ring, bf),
            pltpu.VMEM(tail, bf), pltpu.VMEM(tail, bf),
            pltpu.VMEM((EARLY, 2, 32, HR, LANES), bf), pltpu.VMEM((EARLY, 2, 32, HR, LANES), bf),
            pltpu.VMEM(tail, f32), pltpu.VMEM(tail, f32),
            dma,
            dma((4, 2)), dma((4, 2)),
            dma((2, 3)), dma((2, 3)),
            dma((CHUNKS, 2, 3)), dma((CHUNKS, 2, 3)),
            dma((CHUNKS, 4, 2)), dma((CHUNKS, 4, 2)),
            dma((CHUNKS, 2)), dma((CHUNKS, 2)),
            dma((EARLY, 2)), dma((EARLY, 2)),
            dma((CHUNKS, 2)), dma((CHUNKS, 2)),
        ],
        compiler_params=pltpu.CompilerParams(
            collective_id=0, has_side_effects=True, vmem_limit_bytes=54 * 1024 * 1024
        ),
    )(counts, panels.reshape(16, 128, 512), src_block, dest_owner.reshape(1, -1), target.reshape(1, -1))
    return parent - sums


def solution(mesh):
    placed = (
        P("col", None, "grp", None),
        P("col", "grp", None),
        P("col", None),
        P("col", None),
        P("col"),
        P("col"),
    )
    return jax.shard_map(
        per_device, mesh=mesh, in_specs=placed, out_specs=P("col", "grp", None), check_vma=False
    )
```

time: 391 us -> 124 us (0.32)
  waiting for transfers between devices: 250 us -> 0 us
  Pallas kernels: 0 us -> 121 us
  local copies, waits for them, and re-layouts: 66.4 us -> 0.01 us
  starting transfers between devices: 22.9 us -> 0 us
  matrix products: 22.8 us -> 0 us
  between operations: 14.1 us -> 0.76 us
  other arithmetic: 10.9 us -> 2.4 us
    all_to_all x2 -> x0, waiting for transfers between devices: 183 us -> none  [the longest x1 183 us: per_device(): lax.all_to_all(buffer, 'col', split_axis=0, concat_axis=0, tiled=True)]
    pallas_call x0 -> x1, Pallas kernels: none -> 121 us  [per_device(): pl.pallas_call(assemble_kernel, out_shape=jax.ShapeDtypeStruct((4, 128, 5...]
    all_gather x1 -> x0, waiting for transfers between devices: 66.1 us -> none  [per_device(): lax.all_gather(panels, 'grp', axis=2, tiled=True)]
    gather x6 -> x0, local copies, waits for them, and re-layouts: 46.5 us -> none  [the longest x4 33.6 us: pair_products(): right_rows = piece_rows[:, lower_table]]
    all_to_all x2 -> x0, starting transfers between devices: 22.9 us -> none  [the longest x1 11.9 us: per_device(): lax.all_to_all(routed, 'col', split_axis=0, concat_axis=0, tiled=True)]
    dot_general x2 -> x0, matrix products: 22.8 us -> none  [the longest x1 12.3 us: assemble(): jnp.einsum('tn,nrc->trc', select, arrived, preferred_element_type=jnp.flo...]
    scatter x2 -> x0, local copies, waits for them, and re-layouts: 14.9 us -> none  [the longest x1 14.1 us: pack_updates(): buffer = jnp.zeros((peer_count * capacity,) + picked.shape[1:], picked.dt...]
    select_n x3 -> x0, other arithmetic: 5.95 us -> none  [the longest x1 5.28 us: pack_updates(): picked = jnp.where(is_live[:, None, None], picked, jnp.zeros_like(picked))]
  transfers between devices with their start and end apart: 3 -> 0, of which waited for: 2 -> 0; matrix products, arithmetic and copies ran while one was open for 22% -> 0% of each run, Pallas kernels for 0% -> 0%
where the time goes in v2:
time: 124 us
  Pallas kernels  121 us (98%)
  other arithmetic  2.4 us (2%)
    pallas_call x1, Pallas kernels, per_device(): pl.pallas_call(assemble_kernel, out_shape=jax.ShapeDtypeStruct((4, 128, 5...  121 us

profile of v2, /device:TPU:24, one launch (start us, length us, event | category | flops | bytes accessed | tf_op | source)
XLA Modules:
  0.0 124.1 jit_solution(16213012049754875357)
XLA Ops:
  0.0 0.0 copy-start
  0.7 121.0 %shard_map.64 = f32[4,128,512]{2,1,0:T(8,128)} custom-call(s32[1]{0:T(128)S(6)} %copy.7.counts, bf16[16,128,512]{2,1,0:T(8,128)(2,1)} %bitcast.3, s32[1,40]{1,0:T(1,128)} %src.1, s32[1,40]{1,0:T(1,128)} %bitcast.4, s32[1,40]{1,0:T(1,128)} %bitcast.5), custom_call_target="tpu_custom_call" | custom-call | tf_op jit(solution)/shard_map/pallas_call | solution.py:405
  121.7 0.0 copy-done
  121.7 2.4 %sub.3 = f32[4,128,512]{2,1,0:T(8,128)} subtract(f32[4,128,512]{2,1,0:T(8,128)S(1)} %copy-done, f32[4,128,512]{2,1,0:T(8,128)} %shard_map.64) | non-fusion elementwise | flops 262144 | bytes 3145728 | tf_op jit(solution)/shard_map/sub | solution.py:436
Async XLA Ops:
  0.0 121.7 %copy-start = (f32[4,128,512]{2,1,0:T(8,128)S(1)}, f32[4,128,512]{2,1,0:T(8,128)}, u32[]{:S(2)}) copy-start(f32[4,128,512]{2,1,0:T(8,128)} %param.7) | copy-start | bytes 3145732

commit v3 on v2

--- a/solution.py
+++ b/solution.py
@@ -10,15 +10,16 @@
 CHUNKS = 16
 HR = 16
 LANES = 128
-EARLY_FROM, EARLY_STEP = 5, 3
-EARLY = (CHUNKS - 1 - EARLY_FROM) // EARLY_STEP + 1
-EARLY_GAP, LAST_GAP = 2, 2
+EARLY_FROM, EARLY_END, EARLY_STEP = 6, 13, 3
+EARLY = (EARLY_END - 1 - EARLY_FROM) // EARLY_STEP + 1
+EARLY_GAP, RING, LAST_GAP = 3, 5, 4
 UNROLL = 8
-GROUP_TICK = (None, 1, 3, 5, 7, 8)
+GROUP_AT = (None, (1, 2), (4, 2), (6, 1), (8, 2), (9, 3))
 
 
 def is_early(c):
-    return jnp.logical_and(lax.rem(c + EARLY_STEP * CHUNKS - EARLY_FROM, EARLY_STEP) == 0, c >= EARLY_FROM)
+    turn = lax.rem(c + EARLY_STEP * CHUNKS - EARLY_FROM, EARLY_STEP) == 0
+    return jnp.logical_and(turn, jnp.logical_and(c >= EARLY_FROM, c < EARLY_END))
 
 
 def assemble_kernel(
@@ -339,12 +340,17 @@
                 def _():
                     z_step(c, s, early)
 
+            for k in range(1, 6):
+                @pl.when(jnp.logical_and(t == GROUP_AT[k][0], s == GROUP_AT[k][1]))
+                def _():
+                    group(k)
+
             return carry
 
         lax.fori_loop(0, 4, inner, 0)
 
         for early in (False, True):
-            done = t - 4 - EARLY_GAP * early
+            done = t - RING - EARLY_GAP * early
 
             @pl.when(within(done, early))
             def _():
@@ -354,14 +360,9 @@
             def _():
                 finish(done - LAST_GAP, early)
 
-        for k in range(1, 6):
-            @pl.when(t == GROUP_TICK[k])
-            def _():
-                group(k)
-
         return carry
 
-    lax.fori_loop(0, CHUNKS + 4 + EARLY_GAP + LAST_GAP, tick, 0)
+    lax.fori_loop(0, CHUNKS + RING + EARLY_GAP + LAST_GAP, tick, 0)
 
     for h in range(2):
         for k in range(3):
@@ -430,7 +431,7 @@
             dma((CHUNKS, 2)), dma((CHUNKS, 2)),
         ],
         compiler_params=pltpu.CompilerParams(
-            collective_id=0, has_side_effects=True, vmem_limit_bytes=54 * 1024 * 1024
+            collective_id=0, has_side_effects=True, vmem_limit_bytes=49 * 1024 * 1024
         ),
     )(counts, panels.reshape(16, 128, 512), src_block, dest_owner.reshape(1, -1), target.reshape(1, -1))
     return parent - sums

time: 124 us -> 121 us (0.976)
  Pallas kernels: 121 us -> 115 us
  local copies, waits for them, and re-layouts: 0.01 us -> 3.55 us
    pallas_call x1, Pallas kernels: 121 us -> 115 us  [per_device(): pl.pallas_call(assemble_kernel, out_shape=jax.ShapeDtypeStruct((4, 128, 5...]
    unnamed x2 -> x10, local copies, waits for them, and re-layouts: 0.01 us -> 3.55 us
where the time goes in v3:
time: 121 us
  Pallas kernels  115 us (95%)
  local copies, waits for them, and re-layouts  3.55 us (3%)
    pallas_call x1, Pallas kernels, per_device(): pl.pallas_call(assemble_kernel, out_shape=jax.ShapeDtypeStruct((4, 128, 5...  115 us
    unnamed x10, local copies, waits for them, and re-layouts  3.55 us

profile of v3, /device:TPU:24, one launch (start us, length us, event | category | flops | bytes accessed | tf_op | source)
XLA Modules:
  0.0 120.9 jit_solution(12611282364271747131)
XLA Ops:
  0.7 0.0 copy-start
  0.7 1.6 %copy-done = bf16[4,4,128,512]{3,2,1,0:T(8,128)(2,1)S(1)} copy-done((bf16[4,4,128,512]{3,2,1,0:T(8,128)(2,1)S(1)}, bf16[4,4,128,512]{3,2,1,0:T(8,128)(2,1)}, u32[]{:S(2)}) %copy-start) | copy-done | bytes 2097176
  2.2 0.0 copy-start.1
  2.2 0.7 copy-done.1
  2.9 0.0 copy-start.2
  2.9 0.7 copy-done.2
  3.6 0.0 copy-start.3
  3.6 0.7 copy-done.3
  4.2 0.0 copy-start.4
  4.2 115.5 %shard_map.64 = f32[4,128,512]{2,1,0:T(8,128)S(1)} custom-call(s32[1]{0:T(128)S(6)} %copy.7.counts, bf16[16,128,512]{2,1,0:T(8,128)(2,1)S(1)} %bitcast.3, s32[1,40]{1,0:T(1,128)S(1)} %copy-done.1, s32[1,40]{1,0:T(1,128)S(1)} %bitcast.4, s32[1,40]{1,0:T(1,128)S(1)} %bitcast.5), custom_call_target="tpu_custom_call" | custom-call | tf_op jit(solution)/shard_map/pallas_call | solution.py:406
  119.7 0.0 copy-done.4
  119.7 1.2 sub.3
Async XLA Ops:
  0.7 1.6 %copy-start = (bf16[4,4,128,512]{3,2,1,0:T(8,128)(2,1)S(1)}, bf16[4,4,128,512]{3,2,1,0:T(8,128)(2,1)}, u32[]{:S(2)}) copy-start(bf16[4,4,128,512]{3,2,1,0:T(8,128)(2,1)} %param.6) | copy-start | bytes 6291460
  2.2 0.7 copy-start.1
  2.9 0.7 copy-start.2
  3.6 0.7 copy-start.3
  4.2 115.5 %copy-start.4 = (f32[4,128,512]{2,1,0:T(8,128)S(1)}, f32[4,128,512]{2,1,0:T(8,128)}, u32[]{:S(2)}) copy-start(f32[4,128,512]{2,1,0:T(8,128)} %param.7) | copy-start | bytes 3145732

commit v4 on v3

--- a/solution.py
+++ b/solution.py
@@ -12,7 +12,7 @@
 LANES = 128
 EARLY_FROM, EARLY_END, EARLY_STEP = 6, 13, 3
 EARLY = (EARLY_END - 1 - EARLY_FROM) // EARLY_STEP + 1
-EARLY_GAP, RING, LAST_GAP = 3, 5, 4
+EARLY_GAP, RING, LAST_GAP = 2, 4, 4
 UNROLL = 8
 GROUP_AT = (None, (1, 2), (4, 2), (6, 1), (8, 2), (9, 3))
 
@@ -50,6 +50,22 @@
              second[0][1], second[0][-1], second[1][1], second[1][-1]]
     for peer in peers:
         pl.semaphore_signal(barrier, inc=1, device_id=peer, device_id_type=MESH)
+
+    pl.semaphore_wait(barrier, len(peers))
+
+    def rcopy(src, dst, ss, rs, who):
+        return pltpu.make_async_remote_copy(
+            src_ref=src, dst_ref=dst, send_sem=ss, recv_sem=rs, device_id=who, device_id_type=MESH
+        )
+
+    def y_copy(q, side):
+        dst = (ups if side == 0 else downs)[q]
+        return rcopy(panels.at[:, q * 32:(q + 1) * 32, :], dst, y_ss.at[q, side], y_rs.at[q, side],
+                     y_side[-1] if side == 0 else y_side[1])
+
+    for q in range(4):
+        for side in range(2):
+            y_copy(q, side).start()
 
     slots = src.shape[1]
     i32 = jnp.int32
@@ -87,17 +103,6 @@
     )
     lab[...] = jnp.broadcast_to(labels, (LANES, LANES)).reshape(2, 4, 16, LANES)
 
-    pl.semaphore_wait(barrier, len(peers))
-
-    def rcopy(src, dst, ss, rs, who):
-        return pltpu.make_async_remote_copy(
-            src_ref=src, dst_ref=dst, send_sem=ss, recv_sem=rs, device_id=who, device_id_type=MESH
-        )
-
-    def y_copy(q, side):
-        dst = (ups if side == 0 else downs)[q]
-        return rcopy(panels.at[:, q * 32:(q + 1) * 32, :], dst, y_ss.at[q, side], y_rs.at[q, side],
-                     y_side[-1] if side == 0 else y_side[1])
 
     def x1_who(h, k):
         return (sib, partner[h][0], partner[h][1])[k]
@@ -133,9 +138,6 @@
 
         lax.fori_loop(0, 16, one, 0)
 
-    for q in range(4):
-        for side in range(2):
-            y_copy(q, side).start()
     for h in range(2):
         for k in range(3):
             lab_copy(h, k).start()

time: 121 us -> 121 us (level)
  no operation moved by 1% of the time
where the time goes in v4:
time: 121 us
  Pallas kernels  116 us (96%)
  local copies, waits for them, and re-layouts  3.55 us (3%)
    pallas_call x1, Pallas kernels, per_device(): pl.pallas_call(assemble_kernel, out_shape=jax.ShapeDtypeStruct((4, 128, 5...  116 us
    unnamed x10, local copies, waits for them, and re-layouts  3.55 us

profile of v4, /device:TPU:24, one launch (start us, length us, event | category | flops | bytes accessed | tf_op | source)
XLA Modules:
  0.0 121.2 jit_solution(12118029671945485447)
XLA Ops:
  0.7 0.0 copy-start
  0.7 1.6 %copy-done = bf16[4,4,128,512]{3,2,1,0:T(8,128)(2,1)S(1)} copy-done((bf16[4,4,128,512]{3,2,1,0:T(8,128)(2,1)S(1)}, bf16[4,4,128,512]{3,2,1,0:T(8,128)(2,1)}, u32[]{:S(2)}) %copy-start) | copy-done | bytes 2097176
  2.2 0.0 copy-start.1
  2.2 0.7 copy-done.1
  2.9 0.0 copy-start.2
  2.9 0.7 copy-done.2
  3.6 0.0 copy-start.3
  3.6 0.7 copy-done.3
  4.2 0.0 copy-start.4
  4.2 115.8 %shard_map.64 = f32[4,128,512]{2,1,0:T(8,128)S(1)} custom-call(s32[1]{0:T(128)S(6)} %copy.7.counts, bf16[16,128,512]{2,1,0:T(8,128)(2,1)S(1)} %bitcast.3, s32[1,40]{1,0:T(1,128)S(1)} %copy-done.1, s32[1,40]{1,0:T(1,128)S(1)} %bitcast.4, s32[1,40]{1,0:T(1,128)S(1)} %bitcast.5), custom_call_target="tpu_custom_call" | custom-call | tf_op jit(solution)/shard_map/pallas_call | solution.py:408
  120.0 0.0 copy-done.4
  120.0 1.2 sub.3
Async XLA Ops:
  0.7 1.6 %copy-start = (bf16[4,4,128,512]{3,2,1,0:T(8,128)(2,1)S(1)}, bf16[4,4,128,512]{3,2,1,0:T(8,128)(2,1)}, u32[]{:S(2)}) copy-start(bf16[4,4,128,512]{3,2,1,0:T(8,128)(2,1)} %param.6) | copy-start | bytes 6291460
  2.2 0.7 copy-start.1
  2.9 0.7 copy-start.2
  3.6 0.7 copy-start.3
  4.2 115.8 %copy-start.4 = (f32[4,128,512]{2,1,0:T(8,128)S(1)}, f32[4,128,512]{2,1,0:T(8,128)}, u32[]{:S(2)}) copy-start(f32[4,128,512]{2,1,0:T(8,128)} %param.7) | copy-start | bytes 3145732
